TPU v7x, 32 devices: a whole 2x2x4 slice. The times are simulated.
32 devices in a mesh: dp: 4 (over y, x), tensor: 8 (over z, core).
Axes of the slice: x: 2, y: 2, z: 4, core: 2. Of those that a mesh axis runs over, the one named last changes fastest.
Arguments:
- layer_input: bfloat16 [8192, 2048], P(('dp', 'tensor')), may hold values from -6 to 6
- segment_ids: int32 [8192], P('dp'), may hold values from 0 to 31, never falling along the last dimension, each value on 1 to 512 neighbouring positions
- first_gain: float32 [2048], replicated, may hold values from 0.5 to 1.5
- first_shift: float32 [2048], replicated, may hold values from -3 to 3
- qkv_weight: bfloat16 [3, 2048, 2048], P(None, 'dp', 'tensor'), may hold values from -0.125 to 0.125
- query_value_bias: float32 [2, 2048], P(None, 'tensor'), may hold values from -3 to 3
- dense_weight: bfloat16 [2048, 2048], P('tensor', 'dp'), may hold values from -0.5 to 0.5
- dense_bias: float32 [2048], replicated, may hold values from -2 to 2
- second_gain: float32 [2048], replicated, may hold values from 0.5 to 1.5
- second_shift: float32 [2048], replicated, may hold values from -3 to 3
- up_weight: bfloat16 [2048, 8192], P('dp', 'tensor'), may hold values from -0.125 to 0.125
- up_bias: float32 [8192], P('tensor'), may hold values from -3 to 3
- down_weight: bfloat16 [8192, 2048], P('tensor', 'dp'), may hold values from -0.0625 to 0.0625
- down_bias: float32 [2048], replicated, may hold values from -2 to 2
- out_grad: bfloat16 [8192, 2048], P(('dp', 'tensor')), may hold values from -6 to 6
Outputs:
- layer_out: bfloat16 [8192, 2048], P(('dp', 'tensor'))
- input_grad: float32 [8192, 2048], P(('dp', 'tensor'))
- first_gain_grad: float32 [2048], replicated
- first_shift_grad: float32 [2048], replicated
- qkv_weight_grad: float32 [3, 2048, 2048], P(None, 'dp', 'tensor')
- query_value_bias_grad: float32 [2, 2048], P(None, 'tensor')
- dense_weight_grad: float32 [2048, 2048], P('tensor', 'dp')
- dense_bias_grad: float32 [2048], replicated
- second_gain_grad: float32 [2048], replicated
- second_shift_grad: float32 [2048], replicated
- up_weight_grad: float32 [2048, 8192], P('dp', 'tensor')
- up_bias_grad: float32 [8192], P('tensor')
- down_weight_grad: float32 [8192, 2048], P('tensor', 'dp')
- down_bias_grad: float32 [2048], replicated
Inputs may be any that keep to these rules, and one draw needn't show every extreme that they name: `segment_ids`: segment numbers never fall along the whole array; a run of equal numbers is one document of at most 512 tokens, and some document has exactly that many.
All inputs are finite; a program needn't handle non-finite values.
Results may differ from a plain program's by a relative error of at most 0.014.
Values may be sent and summed in bfloat16 or wider, within the bound.
A program may use at most 256 MiB of HBM per device.

v0:
```python
from functools import partial
import math

import jax
import jax.numpy as jnp
from jax import lax
from jax.sharding import PartitionSpec as P

HEADS = 32
HEAD_DIM = 64


EPSILON = 1e-05
NEG_FILL = -1e30


def layer_norm(source_rows, norm_gain, norm_shift):
    centre = jnp.mean(source_rows, axis=1, keepdims=True)
    centred = source_rows - centre
    inv_std = lax.rsqrt(jnp.mean(centred * centred, axis=1, keepdims=True) + EPSILON)
    unit_rows = centred * inv_std
    return (unit_rows * norm_gain + norm_shift, unit_rows, inv_std)


def norm_backward(grad_out, unit_rows, inv_std, norm_gain):
    scaled = grad_out * norm_gain
    grad_rows = inv_std * (
        scaled
        - jnp.mean(scaled, axis=1, keepdims=True)
        - unit_rows * jnp.mean(scaled * unit_rows, axis=1, keepdims=True)
    )
    return (grad_rows, jnp.sum(grad_out * unit_rows, axis=0), jnp.sum(grad_out, axis=0))


def whole_rows(normed):
    return lax.all_gather(normed, "tensor", axis=0, tiled=True)


def summed_rows(source, weight):
    return lax.psum_scatter(
        jnp.dot(source, weight, preferred_element_type=jnp.float32),
        "tensor",
        scatter_dimension=0,
        tiled=True,
    )


def input_rows(grad_whole, weight):
    return lax.psum_scatter(
        lax.dot_general(
            grad_whole, weight, (((1,), (1,)), ((), ())), preferred_element_type=jnp.float32
        ),
        "tensor",
        scatter_dimension=0,
        tiled=True,
    )


def weight_and_input(grad_local, kept, weight):
    shard_rows = lax.all_gather(grad_local, "tensor", axis=0, tiled=True)
    weight_grad = lax.dot_general(
        kept, shard_rows, (((0,), (0,)), ((), ())), preferred_element_type=jnp.float32
    )
    part_grad = lax.dot_general(
        shard_rows, weight, (((1,), (1,)), ((), ())), preferred_element_type=jnp.float32
    )
    return (weight_grad, part_grad)


def window_bounds(seq_len, block_len, first_row):
    window_len = min(seq_len, block_len + seq_len // 4)
    key_start = jnp.clip(first_row + block_len - window_len, 0, seq_len - window_len)
    return (window_len, key_start)


def block_scores(query_rows, key_heads, key_segs, key_start, query_seg, first_row, slopes, factor):
    block_len = query_rows.shape[0]
    window_len = key_heads.shape[0]
    raw_scores = (
        jnp.einsum("bhe,khe->hbk", query_rows, key_heads, preferred_element_type=jnp.float32)
        * factor
    )
    key_pos = key_start + jnp.arange(window_len, dtype=jnp.int32)
    query_pos = first_row + jnp.arange(block_len, dtype=jnp.int32)
    distance = (query_pos[:, None] - key_pos[None, :]).astype(jnp.float32)
    scores = raw_scores - slopes[:, None, None] * distance[None]
    allowed = (query_seg[:, None] == key_segs[None, :]) & (key_pos[None, :] <= query_pos[:, None])
    return jnp.where(allowed[None], scores, NEG_FILL)


def attention_forward(query_all, key_all, value_all, segments, slopes):
    seq_len, col_width = query_all.shape
    head_count = col_width // HEAD_DIM
    block_len = min(512, seq_len)
    factor = 1.0 / math.sqrt(HEAD_DIM)

    def one_block(block_id):
        first_row = block_id * block_len
        window_len, key_start = window_bounds(seq_len, block_len, first_row)
        query_rows = lax.dynamic_slice_in_dim(query_all, first_row, block_len, 0).reshape(
            block_len, head_count, HEAD_DIM
        )
        key_heads = lax.dynamic_slice_in_dim(key_all, key_start, window_len, 0).reshape(
            window_len, head_count, HEAD_DIM
        )
        value_heads = lax.dynamic_slice_in_dim(value_all, key_start, window_len, 0).reshape(
            window_len, head_count, HEAD_DIM
        )
        key_segs = lax.dynamic_slice_in_dim(segments, key_start, window_len)
        query_seg = lax.dynamic_slice_in_dim(segments, first_row, block_len)
        scores = block_scores(
            query_rows, key_heads, key_segs, key_start, query_seg, first_row, slopes, factor
        )
        highest = jnp.max(scores, axis=2, keepdims=True)
        exponent = jnp.exp(scores - highest)
        row_total = jnp.sum(exponent, axis=2, keepdims=True)
        weights = (exponent / row_total).astype(jnp.bfloat16)
        mixed_rows = jnp.einsum(
            "hbk,khe->bhe", weights, value_heads, preferred_element_type=jnp.float32
        )
        return (mixed_rows.reshape(block_len, col_width), (highest + jnp.log(row_total))[:, :, 0])

    mixed_rows, log_sums = lax.map(one_block, jnp.arange(seq_len // block_len, dtype=jnp.int32))
    return (mixed_rows.reshape(seq_len, col_width), log_sums)


def attention_backward(query_all, key_all, value_all, head_grad, segments, slopes, log_sums):
    seq_len, col_width = query_all.shape
    head_count = col_width // HEAD_DIM
    block_len = min(512, seq_len)
    factor = 1.0 / math.sqrt(HEAD_DIM)

    def one_block(running, block_id):
        key_grad, value_grad = running
        first_row = block_id * block_len
        window_len, key_start = window_bounds(seq_len, block_len, first_row)
        query_rows = lax.dynamic_slice_in_dim(query_all, first_row, block_len, 0).reshape(
            block_len, head_count, HEAD_DIM
        )
        grad_rows = lax.dynamic_slice_in_dim(head_grad, first_row, block_len, 0).reshape(
            block_len, head_count, HEAD_DIM
        )
        key_heads = lax.dynamic_slice_in_dim(key_all, key_start, window_len, 0).reshape(
            window_len, head_count, HEAD_DIM
        )
        value_heads = lax.dynamic_slice_in_dim(value_all, key_start, window_len, 0).reshape(
            window_len, head_count, HEAD_DIM
        )
        key_segs = lax.dynamic_slice_in_dim(segments, key_start, window_len)
        query_seg = lax.dynamic_slice_in_dim(segments, first_row, block_len)
        scores = block_scores(
            query_rows, key_heads, key_segs, key_start, query_seg, first_row, slopes, factor
        )
        probs = jnp.exp(scores - log_sums[block_id][:, :, None])
        weights = probs.astype(jnp.bfloat16)
        value_part = jnp.einsum(
            "hbk,bhe->khe", weights, grad_rows, preferred_element_type=jnp.float32
        ).reshape(window_len, col_width)
        prob_grad = jnp.einsum(
            "bhe,khe->hbk", grad_rows, value_heads, preferred_element_type=jnp.float32
        )
        row_inner = jnp.sum(probs * prob_grad, axis=2, keepdims=True)
        score_grad = (probs * (prob_grad - row_inner)).astype(jnp.bfloat16)
        query_grad = (
            jnp.einsum("hbk,khe->bhe", score_grad, key_heads, preferred_element_type=jnp.float32)
            * factor
        )
        key_part = (
            jnp.einsum("hbk,bhe->khe", score_grad, query_rows, preferred_element_type=jnp.float32)
            * factor
        ).reshape(window_len, col_width)
        key_grad = lax.dynamic_update_slice_in_dim(
            key_grad,
            lax.dynamic_slice_in_dim(key_grad, key_start, window_len, 0) + key_part,
            key_start,
            0,
        )
        value_grad = lax.dynamic_update_slice_in_dim(
            value_grad,
            lax.dynamic_slice_in_dim(value_grad, key_start, window_len, 0) + value_part,
            key_start,
            0,
        )
        return ((key_grad, value_grad), query_grad.reshape(block_len, col_width))

    zero_grads = jnp.zeros((seq_len, col_width), jnp.float32)
    (key_grad, value_grad), query_grad = lax.scan(
        one_block, (zero_grads, zero_grads), jnp.arange(seq_len // block_len, dtype=jnp.int32)
    )
    return (query_grad.reshape(seq_len, col_width), key_grad, value_grad)


def shards(
    layer_input,
    segment_ids,
    first_gain,
    first_shift,
    qkv_weight,
    query_value_bias,
    dense_weight,
    dense_bias,
    second_gain,
    second_shift,
    up_weight,
    up_bias,
    down_weight,
    down_bias,
    out_grad,
):
    qkv_full, dense_full, up_full, down_full = (
        lax.all_gather(qkv_weight, "dp", axis=1, tiled=True),
        lax.all_gather(dense_weight, "dp", axis=1, tiled=True),
        lax.all_gather(up_weight, "dp", axis=0, tiled=True),
        lax.all_gather(down_weight, "dp", axis=1, tiled=True),
    )
    model_width = qkv_full.shape[1]
    head_width = qkv_full.shape[2]
    up_width = up_bias.shape[0]
    qkv_cat = jnp.transpose(qkv_full, (1, 0, 2)).reshape(model_width, 3 * head_width)
    inputs = layer_input.astype(jnp.float32)
    normed1, unit_first, inv_first = layer_norm(inputs, first_gain, first_shift)
    whole1 = whole_rows(normed1.astype(jnp.bfloat16))
    zero_bias = jnp.zeros_like(query_value_bias[0])
    bias_cat = jnp.concatenate([query_value_bias[0], zero_bias, query_value_bias[1]])
    projected = (jnp.dot(whole1, qkv_cat, preferred_element_type=jnp.float32) + bias_cat).astype(
        jnp.bfloat16
    )
    query_all = projected[:, :head_width]
    key_all = projected[:, head_width : 2 * head_width]
    value_all = projected[:, 2 * head_width :]
    head_count = head_width // HEAD_DIM
    tensor_pos = lax.axis_index("tensor")
    global_heads = tensor_pos * head_count + jnp.arange(head_count, dtype=jnp.int32)
    slopes = jnp.power(2.0, -8.0 * (global_heads + 1).astype(jnp.float32) / HEADS)
    attended_full, log_sums = attention_forward(query_all, key_all, value_all, segment_ids, slopes)
    attended = attended_full.astype(jnp.bfloat16)
    attn_branch = summed_rows(attended, dense_full)
    residual = inputs + (attn_branch + dense_bias)
    normed2, unit_second, inv_second = layer_norm(residual, second_gain, second_shift)
    whole2 = whole_rows(normed2.astype(jnp.bfloat16))
    pre_act = jnp.dot(whole2, up_full, preferred_element_type=jnp.float32) + up_bias
    activated = jax.nn.gelu(pre_act, approximate=False).astype(jnp.bfloat16)
    mlp_branch = summed_rows(activated, down_full) + down_bias
    layer_out = (residual + mlp_branch).astype(jnp.bfloat16)
    down_grad, act_grad = weight_and_input(out_grad, activated, down_full)
    unused_out, gelu_back = jax.vjp(partial(jax.nn.gelu, approximate=False), pre_act)
    pre_grad = gelu_back(act_grad)[0].astype(jnp.bfloat16)
    up_bias_part = jnp.sum(pre_grad.astype(jnp.float32), axis=0)
    up_grad = lax.dot_general(
        whole2, pre_grad, (((0,), (0,)), ((), ())), preferred_element_type=jnp.float32
    )
    normed2_grad = input_rows(pre_grad, up_full)
    back_second, second_gain_part, second_shift_part = norm_backward(
        normed2_grad, unit_second, inv_second, second_gain
    )
    out_grad_full = out_grad.astype(jnp.float32)
    residual_grad = out_grad_full + back_second
    branch_grad = residual_grad.astype(jnp.bfloat16)
    dense_grad, attended_grad_full = weight_and_input(branch_grad, attended, dense_full)
    attended_grad = attended_grad_full.astype(jnp.bfloat16)
    query_grad, key_grad, value_grad = attention_backward(
        query_all, key_all, value_all, attended_grad, segment_ids, slopes, log_sums
    )
    qkv_grad_cat = jnp.concatenate([query_grad, key_grad, value_grad], axis=1).astype(jnp.bfloat16)
    qkv_sums = jnp.sum(qkv_grad_cat.astype(jnp.float32), axis=0)
    bias_part = jnp.stack([qkv_sums[:head_width], qkv_sums[2 * head_width :]])
    qkv_grad_flat = lax.dot_general(
        whole1, qkv_grad_cat, (((0,), (0,)), ((), ())), preferred_element_type=jnp.float32
    )
    qkv_grad = jnp.transpose(qkv_grad_flat.reshape(model_width, 3, head_width), (1, 0, 2))
    normed1_grad = input_rows(qkv_grad_cat, qkv_cat)
    back_first, first_gain_part, first_shift_part = norm_backward(
        normed1_grad, unit_first, inv_first, first_gain
    )
    input_grad = residual_grad + back_first
    dense_bias_part = jnp.sum(branch_grad.astype(jnp.float32), axis=0)
    down_bias_part = jnp.sum(out_grad_full, axis=0)
    qkv_wgrad, dense_wgrad, up_wgrad, down_wgrad = (
        lax.psum_scatter(
            qkv_grad.astype(jnp.bfloat16), "dp", scatter_dimension=1, tiled=True
        ).astype(jnp.float32),
        lax.psum_scatter(
            dense_grad.astype(jnp.bfloat16), "dp", scatter_dimension=1, tiled=True
        ).astype(jnp.float32),
        lax.psum_scatter(
            up_grad.astype(jnp.bfloat16), "dp", scatter_dimension=0, tiled=True
        ).astype(jnp.float32),
        lax.psum_scatter(
            down_grad.astype(jnp.bfloat16), "dp", scatter_dimension=1, tiled=True
        ).astype(jnp.float32),
    )
    bias_wide = lax.dynamic_update_slice_in_dim(
        jnp.zeros((2, model_width), jnp.float32), bias_part, tensor_pos * head_width, 1
    )
    up_wide = lax.dynamic_update_slice_in_dim(
        jnp.zeros((up_width * lax.axis_size("tensor"),), jnp.float32),
        up_bias_part,
        tensor_pos * up_width,
        0,
    )
    summed_small = lax.psum(
        (
            first_gain_part,
            first_shift_part,
            dense_bias_part,
            second_gain_part,
            second_shift_part,
            down_bias_part,
            bias_wide,
            up_wide,
        ),
        ("dp", "tensor"),
    )
    query_value_grad = lax.dynamic_slice_in_dim(
        summed_small[6], tensor_pos * head_width, head_width, 1
    )
    up_bias_grad = lax.dynamic_slice_in_dim(summed_small[7], tensor_pos * up_width, up_width, 0)
    return (
        layer_out,
        input_grad,
        summed_small[0],
        summed_small[1],
        qkv_wgrad,
        query_value_grad,
        dense_wgrad,
        summed_small[2],
        summed_small[3],
        summed_small[4],
        up_wgrad,
        up_bias_grad,
        down_wgrad,
        summed_small[5],
    )


def solution(mesh):
    placed = (
        P(("dp", "tensor"), None),
        P("dp"),
        P(),
        P(),
        P(None, "dp", "tensor"),
        P(None, "tensor"),
        P("tensor", "dp"),
        P(),
        P(),
        P(),
        P("dp", "tensor"),
        P("tensor"),
        P("tensor", "dp"),
        P(),
        P(("dp", "tensor"), None),
    )
    return jax.shard_map(
        shards,
        mesh=mesh,
        in_specs=placed,
        out_specs=(
            P(("dp", "tensor"), None),
            P(("dp", "tensor"), None),
            P(),
            P(),
            P(None, "dp", "tensor"),
            P(None, "tensor"),
            P("tensor", "dp"),
            P(),
            P(),
            P(),
            P("dp", "tensor"),
            P("tensor"),
            P("tensor", "dp"),
            P(),
        ),
        check_vma=False,
    )
```

profile of v0, /device:TPU:8, one launch (start us, length us, event | category | flops | bytes accessed | tf_op | source)
XLA Modules:
  0.0 1696.0 jit_solution(2553032219274048178)
XLA Ops:
  16.8 38.5 %all-gather.11.cloned.1.call-done = bf16[3,2048,256]{1,2,0:T(8,128)(2,1)} async-done(((bf16[3,512,256]{1,2,0:T(8,128)(2,1)}), bf16[3,2048,256]{1,2,0:T(8,128)(2,1)}) %all-gather.11.cloned.1.call-update) | async-done | bytes 3145744 | tf_op jit(solution)/shard_map/all_gather | solution.py:211
  55.3 81.6 %all-gather.9.cloned.1.call-done = bf16[2048,2048]{1,0:T(8,128)(2,1)} async-done(((bf16[256,2048]{1,0:T(8,128)(2,1)}), bf16[2048,2048]{1,0:T(8,128)(2,1)}) %all-gather.9.cloned.1.call-update) | async-done | bytes 8388624 | tf_op jit(solution)/shard_map/all_gather | solution.py:36
  136.9 10.1 add_convert_fusion.1
  151.5 60.1 %while.36 = (s32[]{:T(128)}, bf16[4,512,256]{2,1,0:T(8,128)(2,1)S(1)}, f32[4,4,512]{2,1,0:T(4,128)}, s32[4]{0:T(128)S(1)}, bf16[2048,256]{0,1:T(8,128)(2,1)}, /*...) while((s32[]{:T(128)}, ...), condition=%wide.region_5.6_spmd.clone, body=%wide.region_2.5_spmd.clone.sunk | while | flops 577240576 | bytes 40997208 | solution.py:123
  162.3 3.4 fusion.99
  177.2 3.4 fusion.99
  192.1 3.4 fusion.99
  207.0 3.4 fusion.99
  211.7 9.7 fusion.38
  222.0 166.0 %reduce-scatter.9.cloned.1.call-done = f32[256,2048]{1,0:T(8,128)} async-done(((f32[2048,2048]{1,0:T(8,128)}), f32[256,2048]{1,0:T(8,128)}) %reduce-scatter.9.cloned.1.call-update) | async-done | bytes 2097168 | tf_op jit(solution)/shard_map/reduce_scatter | solution.py:40
  393.4 50.2 %all-gather.17.cloned.1.call-done = bf16[2048,1024]{1,0:T(8,128)(2,1)} async-done(((bf16[512,1024]{1,0:T(8,128)(2,1)}), bf16[2048,1024]{1,0:T(8,128)(2,1)}) %all-gather.17.cloned.1.call-update) | async-done | bytes 4194320 | tf_op jit(solution)/shard_map/all_gather | solution.py:213
  443.6 81.4 %all-gather.15.cloned.1.call-done = bf16[2048,2048]{1,0:T(8,128)(2,1)} async-done(((bf16[256,2048]{1,0:T(8,128)(2,1)}), bf16[2048,2048]{1,0:T(8,128)(2,1)}) %all-gather.15.cloned.1.call-update) | async-done | bytes 8388624 | tf_op jit(solution)/shard_map/all_gather | solution.py:36
  525.0 14.4 fusion.39
  539.5 41.0 %all-gather.19.cloned.1.call-done = bf16[1024,2048]{1,0:T(8,128)(2,1)} async-done(((bf16[1024,512]{1,0:T(8,128)(2,1)}), bf16[1024,2048]{1,0:T(8,128)(2,1)}) %all-gather.19.cloned.1.call-update) | async-done | bytes 4194320 | tf_op jit(solution)/shard_map/all_gather | solution.py:214
  580.5 81.0 %all-gather.21.cloned.1.call-done = bf16[2048,2048]{1,0:T(8,128)(2,1)} async-done(((bf16[256,2048]{1,0:T(8,128)(2,1)}), bf16[2048,2048]{1,0:T(8,128)(2,1)}) %all-gather.21.cloned.1.call-update) | async-done | bytes 8388624 | tf_op jit(solution)/shard_map/all_gather | solution.py:60
  661.5 33.6 %convert_reduce_fusion = (f32[1024]{0:T(1024)}, bf16[2048,1024]{1,0:T(8,128)(2,1)S(1)}, f32[2048,1024]{1,0:T(8,128)}) fusion(f32[2048,1024]{1,0:T(8,128)} %fusion.39, f32[1024]{0:T(1024)S(1)} %copy-done.27, bf16[2048,2048]{1,0:T(8,128)(2,1)} %all-gather.21.cloned.1.call-done, bf16[1024,2048]{1,0:T(8,128)(2,1)} %all-gather.19.cloned.1.call-done), kind=kOutput, calls=%fused_computation.44 | convolution fusion | flops 8747219968 | bytes 33562624 | tf_op jit(solution)/shard_map/dot_general | solution.py:64
  697.0 11.9 fusion.41
  709.0 10.0 multiply_convert_fusion.1
  719.0 15.3 fusion.40
  734.4 141.2 %reduce-scatter.13.cloned.1.call-done = f32[256,2048]{1,0:T(8,128)} async-done(((f32[2048,2048]{1,0:T(8,128)}), f32[256,2048]{1,0:T(8,128)}) %reduce-scatter.13.cloned.1.call-update) | async-done | bytes 2097168 | tf_op jit(solution)/shard_map/reduce_scatter | solution.py:49
  878.7 165.8 %reduce-scatter.11.cloned.1.call-done = f32[256,2048]{1,0:T(8,128)} async-done(((f32[2048,2048]{1,0:T(8,128)}), f32[256,2048]{1,0:T(8,128)}) %reduce-scatter.11.cloned.1.call-update) | async-done | bytes 2097168 | tf_op jit(solution)/shard_map/reduce_scatter | solution.py:40
  1044.5 6.3 convert_reduce_fusion.4
  1050.9 14.2 convolution_convert_fusion.1
  1065.2 14.1 convolution_convert_fusion
  1079.4 52.2 %all-gather.23.cloned.1.call-done = bf16[2048,2048]{1,0:T(8,128)(2,1)} async-done(((bf16[256,2048]{1,0:T(8,128)(2,1)}), bf16[2048,2048]{1,0:T(8,128)(2,1)}) %all-gather.23.cloned.1.call-update) | async-done | bytes 8388624 | tf_op jit(solution)/shard_map/all_gather | solution.py:60
  1131.6 6.7 convolution_convert_fusion.3
  1138.4 6.8 convolution_convert_fusion.4
  1149.2 161.2 %while.37 = (s32[]{:T(128)}, f32[2048,256]{1,0:T(8,128)}, f32[2048,256]{1,0:T(8,128)}, bf16[4,512,256]{2,1,0:T(8,128)(2,1)}, s32[4]{0:T(128)S(1)}, /*index=5*/bf...) while((s32[]{:T(128)}, f32[2048,256]{1,0:T(8,128)}, ...), condition=%wide.region_15.16_spmd.clone, body=%wide.region_13.15_spmd.clone.sunk | while | flops 1368915456 | bytes 111489488 | solution.py:187
  1170.6 3.8 multiply_reduce_fusion.7
  1181.6 4.1 dynamic_update_slice.73
  1185.7 4.3 dynamic_update_slice.72
  1211.6 3.8 multiply_reduce_fusion.7
  1222.6 4.1 dynamic_update_slice.73
  1226.7 4.3 dynamic_update_slice.72
  1252.0 3.8 multiply_reduce_fusion.7
  1263.0 4.1 dynamic_update_slice.73
  1267.1 4.3 dynamic_update_slice.72
  1292.3 3.8 multiply_reduce_fusion.7
  1303.3 3.5 dynamic_update_slice.73
  1306.8 3.7 dynamic_update_slice.72
  1314.3 10.8 convolution_convert_fusion.2
  1325.1 4.7 copy.49
  1329.9 11.5 fusion.31
  1352.3 22.8 %reduce-scatter.17.cloned.1.call-done = bf16[3,512,256]{2,1,0:T(8,128)(2,1)} async-done(((bf16[3,2048,256]{2,1,0:T(8,128)(2,1)}), bf16[3,512,256]{2,1,0:T(8,128)(2,1)}) %reduce-scatter.17.cloned.1.call-update) | async-done | bytes 786448 | tf_op jit(solution)/shard_map/reduce_scatter | solution.py:279
  1377.5 165.2 %reduce-scatter.15.cloned.1.call-done = f32[256,2048]{1,0:T(8,128)} async-done(((f32[2048,2048]{1,0:T(8,128)}), f32[256,2048]{1,0:T(8,128)}) %reduce-scatter.15.cloned.1.call-update) | async-done | bytes 2097168 | tf_op jit(solution)/shard_map/reduce_scatter | solution.py:49
  1542.7 3.2 fusion.29
  1545.9 3.7 fusion.28
  1549.6 129.4 %all-reduce.3.cloned.1.call-done = (f32[2048]{0:T(1024)}, f32[2048]{0:T(1024)}, f32[2,2048]{1,0:T(2,128)}, f32[2048]{0:T(1024)}, f32[2048]{0:T(1024)}, /*index=5*/f32[2048]{0:T(1024)}, f32[8192]{0:T(1024)}, f32[2048]{0:T(1024)}) async-done(((f32[2048]{0:T(1024)}, f32[2048]{0:T(1024)}, f32[2,2048]{1,0:T(2,128)}, f32[2048]{0:T(1024)}, f32[2048]{0:T(1024)}, /*index=5*/f32[2048]{0:T(1024)}, f32[8192]{0:T(1024)}, ...) | async-done | bytes 98320 | tf_op jit(solution)/shard_map/psum | solution.py:301
  (335 shorter events, 202.6 us)
Async XLA Ops:
  7.2 9.6 copy-start.28
  7.2 48.1 %all-gather.11.cloned.1.call-start = ((), (), s32[]{:S(2)}) async-start(), calls=%async_computation.9 | async-start | bytes 3932160 | tf_op jit(solution)/shard_map/all_gather | solution.py:211
  9.6 127.3 %all-gather.9.cloned.1.call-start = ((), (), s32[]{:S(2)}) async-start(), calls=%async_computation.8 | async-start | bytes 9437184 | tf_op jit(solution)/shard_map/all_gather | solution.py:36
  16.0 195.7 %all-gather.13.cloned.1.call-start = ((), (), s32[]{:S(2)}) async-start(), calls=%async_computation.10 | async-start | bytes 1310720 | tf_op jit(solution)/shard_map/all_gather | solution.py:212
  16.7 371.3 %reduce-scatter.9.cloned.1.call-start = ((), (), s32[]{:S(2)}) async-start(), calls=%async_computation.11 | async-start | bytes 18874368 | tf_op jit(solution)/shard_map/reduce_scatter | solution.py:40
  147.0 4.6 copy-start.13
  211.6 9.7 copy-start.5
  221.3 166.7 %copy-start.3 = (bf16[256,2048]{1,0:T(8,128)(2,1)S(1)}, bf16[256,2048]{1,0:T(8,128)(2,1)}, u32[]{:S(2)}) copy-start(bf16[256,2048]{1,0:T(8,128)(2,1)} %param.19) | copy-start | bytes 3145732
  221.3 166.7 %copy-start.23 = (f32[2048]{0:T(1024)S(1)}, f32[2048]{0:T(1024)}, u32[]{:S(2)}) copy-start(f32[2048]{0:T(1024)} %param.26) | copy-start | bytes 24580
  221.4 169.0 %copy-start.16 = (f32[2048]{0:T(1024)S(1)}, f32[2048]{0:T(1024)}, u32[]{:S(2)}) copy-start(f32[2048]{0:T(1024)} %param.27) | copy-start | bytes 24580
  221.4 169.0 %copy-start.24 = (f32[2048]{0:T(1024)S(1)}, f32[2048]{0:T(1024)}, u32[]{:S(2)}) copy-start(f32[2048]{0:T(1024)} %param.28) | copy-start | bytes 24580
  221.4 222.2 %all-gather.17.cloned.1.call-start = ((), (), s32[]{:S(2)}) async-start(), calls=%async_computation.13 | async-start | bytes 5242880 | tf_op jit(solution)/shard_map/all_gather | solution.py:213
  222.0 303.1 %all-gather.15.cloned.1.call-start = ((), (), s32[]{:S(2)}) async-start(), calls=%async_computation.12 | async-start | bytes 9437184 | tf_op jit(solution)/shard_map/all_gather | solution.py:36
  391.8 188.7 %all-gather.19.cloned.1.call-start = ((), (), s32[]{:S(2)}) async-start(), calls=%async_computation.14 | async-start | bytes 5242880 | tf_op jit(solution)/shard_map/all_gather | solution.py:214
  392.6 268.9 %all-gather.21.cloned.1.call-start = ((), (), s32[]{:S(2)}) async-start(), calls=%async_computation.16 | async-start | bytes 9437184 | tf_op jit(solution)/shard_map/all_gather | solution.py:60
  393.3 268.2 %copy-start.27 = (f32[1024]{0:T(1024)S(1)}, f32[1024]{0:T(1024)}, u32[]{:S(2)}) copy-start(f32[1024]{0:T(1024)} %param.30) | copy-start | bytes 12292
  393.3 482.2 %reduce-scatter.13.cloned.1.call-start = ((), (), s32[]{:S(2)}) async-start(), calls=%async_computation.17 | async-start | bytes 18874368 | tf_op jit(solution)/shard_map/reduce_scatter | solution.py:49
  661.5 35.5 %copy-start.29 = (bf16[2048,1024]{1,0:T(8,128)(2,1)S(1)}, bf16[2048,1024]{1,0:T(8,128)(2,1)}, u32[]{:S(2)}) copy-start(bf16[2048,1024]{1,0:T(8,128)(2,1)} %all-gather.17.cloned.1.call-done) | copy-start | bytes 12582916
  708.9 335.5 %reduce-scatter.11.cloned.1.call-start = ((), (), s32[]{:S(2)}) async-start(), calls=%async_computation.15 | async-start | bytes 18874368 | tf_op jit(solution)/shard_map/reduce_scatter | solution.py:40
  734.3 310.1 %copy-start.11 = (bf16[256,2048]{1,0:T(8,128)(2,1)S(1)}, bf16[256,2048]{1,0:T(8,128)(2,1)}, u32[]{:S(2)}) copy-start(bf16[256,2048]{1,0:T(8,128)(2,1)} %param.33) | copy-start | bytes 3145732
  734.3 310.1 %copy-start.25 = (f32[2048]{0:T(1024)S(1)}, f32[2048]{0:T(1024)}, u32[]{:S(2)}) copy-start(f32[2048]{0:T(1024)} %param.32) | copy-start | bytes 24580
  734.4 397.2 %all-gather.23.cloned.1.call-start = ((), (), s32[]{:S(2)}) async-start(), calls=%async_computation.18 | async-start | bytes 9437184 | tf_op jit(solution)/shard_map/all_gather | solution.py:60
  1050.8 291.5 %reduce-scatter.21.cloned.1.call-start = ((), (), s32[]{:S(2)}) async-start(), calls=%async_computation.22 | async-start | bytes 5242880 | tf_op jit(solution)/shard_map/reduce_scatter | solution.py:285
  1065.1 66.5 %copy-start.6 = (bf16[4,512,256]{2,1,0:T(8,128)(2,1)S(1)}, bf16[4,512,256]{2,1,0:T(8,128)(2,1)}, u32[]{:S(2)}) copy-start(bf16[4,512,256]{2,1,0:T(8,128)(2,1)} %copy-done.5) | copy-start | bytes 3145732
  1065.1 280.1 %reduce-scatter.23.cloned.1.call-start = ((), (), s32[]{:S(2)}) async-start(), calls=%async_computation.23 | async-start | bytes 5242880 | tf_op jit(solution)/shard_map/reduce_scatter | solution.py:288
  1079.3 271.1 %reduce-scatter.19.cloned.1.call-start = ((), (), s32[]{:S(2)}) async-start(), calls=%async_computation.21 | async-start | bytes 1310720 | tf_op jit(solution)/shard_map/reduce_scatter | solution.py:282
  1079.4 59.0 %copy-start.12 = (bf16[256,2048]{1,0:T(8,128)(2,1)S(1)}, bf16[256,2048]{1,0:T(8,128)(2,1)}, u32[]{:S(2)}) copy-start(bf16[256,2048]{1,0:T(8,128)(2,1)} %all-gather.13.cloned.1.call-done) | copy-start | bytes 3145732
  1138.3 10.9 copy-start.14
  1138.4 236.8 %reduce-scatter.17.cloned.1.call-start = ((), (), s32[]{:S(2)}) async-start(), calls=%async_computation.20 | async-start | bytes 3932160 | tf_op jit(solution)/shard_map/reduce_scatter | solution.py:279
  1168.2 2.4 copy-start.2
  1176.7 2.3 copy-start
  1209.2 2.4 copy-start.2
  1217.6 2.3 copy-start
  1249.6 2.4 copy-start.2
  1258.1 2.3 copy-start
  1289.9 2.4 copy-start.2
  1310.4 3.9 copy-start.10
  1312.2 17.7 %copy-start.8 = (bf16[2048,256]{1,0:T(8,128)(2,1)}, bf16[2048,256]{1,0:T(8,128)(2,1)S(1)}, u32[]{:S(2)}) copy-start(bf16[2048,256]{1,0:T(8,128)(2,1)S(1)} %convert.11) | copy-start | bytes 3145732
  1314.3 15.6 copy-start.9
  1329.8 212.9 %reduce-scatter.15.cloned.1.call-start = ((), (), s32[]{:S(2)}) async-start(), calls=%async_computation.19 | async-start | bytes 18874368 | tf_op jit(solution)/shard_map/reduce_scatter | solution.py:49
  1341.4 337.6 %all-reduce.3.cloned.1.call-start = ((), (), s32[]{:S(2)}) async-start(), calls=%async_computation.24 | async-start | bytes 196608 | tf_op jit(solution)/shard_map/psum | solution.py:301
  1342.2 35.3 %copy-start.15 = (f32[8192]{0:T(1024)}, f32[8192]{0:T(1024)S(1)}, u32[]{:S(2)}) copy-start(f32[8192]{0:T(1024)S(1)} %dynamic_update_slice.54) | copy-start | bytes 98308
  1342.2 200.5 %copy-start.4 = (bf16[256,2048]{1,0:T(8,128)(2,1)S(1)}, bf16[256,2048]{1,0:T(8,128)(2,1)}, u32[]{:S(2)}) copy-start(bf16[256,2048]{1,0:T(8,128)(2,1)} %param.19) | copy-start | bytes 3145732
  1342.2 200.5 %copy-start.17 = (f32[2048]{0:T(1024)S(1)}, f32[2048]{0:T(1024)}, u32[]{:S(2)}) copy-start(f32[2048]{0:T(1024)} %param.21) | copy-start | bytes 24580
  1342.2 200.5 %copy-start.20 = (f32[256]{0:T(256)S(1)}, f32[256]{0:T(256)}, u32[]{:S(2)}) copy-start(f32[256]{0:T(256)} %copy-done.19) | copy-start | bytes 3076
  1342.2 200.5 %copy-start.22 = (f32[256]{0:T(256)S(1)}, f32[256]{0:T(256)}, u32[]{:S(2)}) copy-start(f32[256]{0:T(256)} %copy-done.21) | copy-start | bytes 3076
  1345.2 200.8 %copy-start.7 = (f32[256,2048]{1,0:T(8,128)S(1)}, f32[256,2048]{1,0:T(8,128)}, u32[]{:S(2)}) copy-start(f32[256,2048]{1,0:T(8,128)} %get-tuple-element.590) | copy-start | bytes 6291460
  1350.4 195.5 %copy-start.18 = (f32[2,2048]{1,0:T(2,128)}, f32[2,2048]{1,0:T(2,128)S(1)}, u32[]{:S(2)}) copy-start(f32[2,2048]{1,0:T(2,128)S(1)} %maximum_dynamic-update-slice_fusion) | copy-start | bytes 49156
  (9 other events, 12.1 us)
Sparse Core Ops, SparseCore 0:
  10.4 44.8 all-gather.10
  57.5 79.3 all-gather.8
  138.7 27.5 all-gather.12
  221.5 166.4 reduce-scatter.8
  389.7 53.8 all-gather.16
  445.6 79.3 all-gather.14
  526.9 53.5 all-gather.18
  582.1 79.3 all-gather.20
  709.0 166.4 reduce-scatter.12
  877.8 166.6 reduce-scatter.10
  1050.9 80.6 all-gather.22
  1134.4 53.7 reduce-scatter.20
  1191.2 52.6 reduce-scatter.22
  1246.6 27.9 reduce-scatter.18
  1330.0 45.0 reduce-scatter.16
  1377.3 165.3 reduce-scatter.14
  1550.1 128.8 all-reduce.2
where the time goes:
time: 1710 us; the launch traced here: 1700 us
  waiting for transfers between devices  1220 us (71%)
  matrix products  221 us (13%)
  local copies, waits for them, and re-layouts  146 us (9%)
  other arithmetic  80 us (5%)
    reduce_scatter x2, waiting for transfers between devices, summed_rows(): lax.psum_scatter(jnp.dot(source, weight, preferred_element_type=jnp.float...  332 us
    reduce_scatter x2, waiting for transfers between devices, input_rows(): lax.psum_scatter(lax.dot_general(grad_whole, weight, (((1,), (1,)), ((),...  306 us
    all_gather x2, waiting for transfers between devices, whole_rows(): return lax.all_gather(normed, 'tensor', axis=0, tiled=True)  163 us
    all_gather x2, waiting for transfers between devices, weight_and_input(): shard_rows = lax.all_gather(grad_local, 'tensor', axis=0, tiled=True)  133 us
    psum x1, waiting for transfers between devices, shards(): lax.psum((first_gain_part, first_shift_part, dense_bias_part, second_gain...  129 us
    all_gather x1, waiting for transfers between devices, shards(): lax.all_gather(up_weight, 'dp', axis=0, tiled=True)  50.2 us
    all_gather x1, waiting for transfers between devices, shards(): lax.all_gather(down_weight, 'dp', axis=1, tiled=True)  41 us
    dot_general x2, matrix products, weight_and_input(): lax.dot_general(shard_rows, weight, (((1,), (1,)), ((), ())), preferred_e...  40.4 us
  transfers between devices with their start and end apart: 17, of which 13 were waited for; matrix products, arithmetic and copies ran while one was open for 22% of the time, Pallas kernels for 0%

commit v1 on v0

v1 whole, which is shorter than its diff:
```python
import functools
import math

import jax
import jax.numpy as jnp
from jax import lax
from jax.experimental import pallas as pl
from jax.experimental.pallas import tpu as pltpu
from jax.sharding import PartitionSpec as P

HEADS = 32
EPSILON = 1e-05
MESH = pl.DeviceIdType.MESH
HEAD_DIM = 64
PAIR = 2 * HEAD_DIM
Q_BLOCK = 256
MASKED = -1e32
NT = (((1,), (1,)), ((), ()))
NN = (((1,), (0,)), ((), ()))


def key_window(seq_len, block):
    width = min(seq_len, Q_BLOCK + seq_len // 4)
    start = jnp.maximum(block * Q_BLOCK + Q_BLOCK - width, 0)
    return width, pl.multiple_of(start, 128)


def masked_distance(seg_row, seg_col, first_query, first_key, width):
    shape = (width, Q_BLOCK)
    key_pos = lax.broadcasted_iota(jnp.int32, shape, 0) + first_key
    query_pos = lax.broadcasted_iota(jnp.int32, shape, 1) + first_query
    delta = key_pos - query_pos
    allowed = (seg_col == seg_row) & (delta <= 0)
    return jnp.where(allowed, delta.astype(jnp.float32), MASKED)


def half_lanes(rows, half):
    lane = lax.broadcasted_iota(jnp.int32, rows.shape, 1)
    return jnp.where((lane < HEAD_DIM) == (half == 0), rows, jnp.zeros_like(rows))


def forward_kernel(slope_ref, proj_ref, seg_row_ref, seg_col_ref, out_ref, lse_ref, value_t, bias_ref):
    seq_len = proj_ref.shape[0]
    width_all = out_ref.shape[1]
    block = pl.program_id(0)

    @pl.when(block == 0)
    def _():
        value_t[...] = proj_ref[:, 2 * width_all :].T

    first = pl.multiple_of(block * Q_BLOCK, Q_BLOCK)
    width, start = key_window(seq_len, block)
    queries = pl.ds(first, Q_BLOCK)
    keys = pl.ds(start, width)
    bias_ref[...] = masked_distance(
        seg_row_ref[:, queries], seg_col_ref[keys, :], first, start, width
    )
    for pair in range(width_all // PAIR):
        cols = pair * PAIR
        query_pair = proj_ref[queries, cols : cols + PAIR] * 0.125
        key_pair = proj_ref[keys, width_all + cols : width_all + cols + PAIR]
        value_pair = value_t[cols : cols + PAIR, keys]
        mixed = []
        for half in range(2):
            head = 2 * pair + half
            scores = lax.dot_general(
                key_pair, half_lanes(query_pair, half), NT, preferred_element_type=jnp.float32
            )
            scores = scores + slope_ref[head] * bias_ref[...]
            highest = jnp.max(scores, axis=0, keepdims=True)
            exponent = jnp.exp(scores - highest)
            total = jnp.sum(exponent, axis=0, keepdims=True)
            part = lax.dot_general(
                value_pair[half * HEAD_DIM : (half + 1) * HEAD_DIM],
                exponent.astype(jnp.bfloat16),
                NN,
                preferred_element_type=jnp.float32,
            )
            mixed.append(part / total)
            lse_ref[head : head + 1, :] = highest + jnp.log(total)
        out_ref[:, cols : cols + PAIR] = jnp.concatenate(mixed, axis=0).T.astype(jnp.bfloat16)


def attention_forward(projected, segments, slopes):
    seq_len, all_cols = projected.shape
    cols = all_cols // 3
    heads = cols // HEAD_DIM
    width = min(seq_len, Q_BLOCK + seq_len // 4)
    return pl.pallas_call(
        forward_kernel,
        grid=(seq_len // Q_BLOCK,),
        in_specs=[
            pl.BlockSpec(memory_space=pltpu.SMEM),
            pl.BlockSpec((seq_len, all_cols), lambda i: (0, 0)),
            pl.BlockSpec((1, seq_len), lambda i: (0, 0)),
            pl.BlockSpec((seq_len, 1), lambda i: (0, 0)),
        ],
        out_specs=[
            pl.BlockSpec((Q_BLOCK, cols), lambda i: (i, 0)),
            pl.BlockSpec((heads, Q_BLOCK), lambda i: (0, i)),
        ],
        out_shape=[
            jax.ShapeDtypeStruct((seq_len, cols), jnp.bfloat16),
            jax.ShapeDtypeStruct((heads, seq_len), jnp.float32),
        ],
        scratch_shapes=[
            pltpu.VMEM((cols, seq_len), jnp.bfloat16),
            pltpu.VMEM((width, Q_BLOCK), jnp.float32),
        ],
        compiler_params=pltpu.CompilerParams(vmem_limit_bytes=40 * 2**20),
        cost_estimate=pl.CostEstimate(flops=4 * seq_len * width * cols, bytes_accessed=6 * seq_len * cols, transcendentals=0),
        name="attention_forward",
    )(slopes, projected, segments[None, :], segments[:, None])


def backward_kernel(slope_ref, proj_ref, grad_ref, lse_ref, seg_row_ref, seg_col_ref, out_ref,
                    key_t, bias_ref, key_sum, value_sum):
    seq_len = proj_ref.shape[0]
    width_all = grad_ref.shape[1]
    block = pl.program_id(0)

    @pl.when(block == 0)
    def _():
        key_t[...] = proj_ref[:, width_all : 2 * width_all].T
        key_sum[...] = jnp.zeros_like(key_sum)
        value_sum[...] = jnp.zeros_like(value_sum)

    first = pl.multiple_of(block * Q_BLOCK, Q_BLOCK)
    width, start = key_window(seq_len, block)
    queries = pl.ds(first, Q_BLOCK)
    keys = pl.ds(start, width)
    bias_ref[...] = masked_distance(
        seg_row_ref[:, queries], seg_col_ref[keys, :], first, start, width
    )
    for pair in range(width_all // PAIR):
        cols = pair * PAIR
        query_pair = proj_ref[queries, cols : cols + PAIR] * 0.125
        key_pair = proj_ref[keys, width_all + cols : width_all + cols + PAIR]
        value_pair = proj_ref[keys, 2 * width_all + cols : 2 * width_all + cols + PAIR]
        grad_pair = grad_ref[queries, cols : cols + PAIR]
        query_grads = []
        key_part = value_part = None
        for half in range(2):
            head = 2 * pair + half
            query_half = half_lanes(query_pair, half)
            grad_half = half_lanes(grad_pair, half)
            scores = lax.dot_general(key_pair, query_half, NT, preferred_element_type=jnp.float32)
            probs = jnp.exp(scores + slope_ref[head] * bias_ref[...] - lse_ref[head : head + 1, queries])
            prob_grad = lax.dot_general(value_pair, grad_half, NT, preferred_element_type=jnp.float32)
            inner = jnp.sum(probs * prob_grad, axis=0, keepdims=True)
            score_grad = (probs * (prob_grad - inner)).astype(jnp.bfloat16)
            value_half = jnp.dot(probs.astype(jnp.bfloat16), grad_half, preferred_element_type=jnp.float32)
            key_half = jnp.dot(score_grad, query_half, preferred_element_type=jnp.float32)
            query_grads.append(
                jnp.dot(
                    key_t[cols + half * HEAD_DIM : cols + (half + 1) * HEAD_DIM, keys],
                    score_grad,
                    preferred_element_type=jnp.float32,
                )
                * 0.125
            )
            value_part = value_half if half == 0 else value_part + value_half
            key_part = key_half if half == 0 else key_part + key_half
        key_sum[keys, cols : cols + PAIR] += key_part
        value_sum[keys, cols : cols + PAIR] += value_part
        out_ref[queries, cols : cols + PAIR] = (
            jnp.concatenate(query_grads, axis=0).T.astype(jnp.bfloat16)
        )

    @pl.when(block == pl.num_programs(0) - 1)
    def _():
        out_ref[:, width_all : 2 * width_all] = key_sum[...].astype(jnp.bfloat16)
        out_ref[:, 2 * width_all :] = value_sum[...].astype(jnp.bfloat16)


def attention_backward(projected, head_grad, segments, slopes, log_sums):
    seq_len, all_cols = projected.shape
    cols = all_cols // 3
    heads = cols // HEAD_DIM
    width = min(seq_len, Q_BLOCK + seq_len // 4)
    return pl.pallas_call(
        backward_kernel,
        grid=(seq_len // Q_BLOCK,),
        in_specs=[
            pl.BlockSpec(memory_space=pltpu.SMEM),
            pl.BlockSpec((seq_len, all_cols), lambda i: (0, 0)),
            pl.BlockSpec((seq_len, cols), lambda i: (0, 0)),
            pl.BlockSpec((heads, seq_len), lambda i: (0, 0)),
            pl.BlockSpec((1, seq_len), lambda i: (0, 0)),
            pl.BlockSpec((seq_len, 1), lambda i: (0, 0)),
        ],
        out_specs=pl.BlockSpec((seq_len, all_cols), lambda i: (0, 0)),
        out_shape=jax.ShapeDtypeStruct((seq_len, all_cols), jnp.bfloat16),
        scratch_shapes=[
            pltpu.VMEM((cols, seq_len), jnp.bfloat16),
            pltpu.VMEM((width, Q_BLOCK), jnp.float32),
            pltpu.VMEM((seq_len, cols), jnp.float32),
            pltpu.VMEM((seq_len, cols), jnp.float32),
        ],
        compiler_params=pltpu.CompilerParams(vmem_limit_bytes=48 * 2**20),
        cost_estimate=pl.CostEstimate(flops=10 * seq_len * width * cols, bytes_accessed=14 * seq_len * cols, transcendentals=0),
        name="attention_backward",
    )(slopes, projected, head_grad, log_sums, segments[None, :], segments[:, None])


ROW_TILE = 16
SUBS = 2


def remote(src, dst, send_sem, recv_sem, peer):
    return pltpu.make_async_remote_copy(
        src_ref=src,
        dst_ref=dst,
        send_sem=send_sem,
        recv_sem=recv_sem,
        device_id={"tensor": peer},
        device_id_type=MESH,
    )


class Line:
    def __init__(self, chips, rows):
        self.chips = chips
        self.sub_rows = rows // SUBS
        self.me = lax.axis_index("tensor")
        self.place = self.me // 2
        self.core = self.me % 2
        self.above = self.me + 2
        self.below = self.me - 2
        self.partner = self.me + 1 - 2 * self.core
        self.has_above = self.place < chips - 1
        self.has_below = self.place > 0

    def rows(self, sub):
        return pl.ds(sub * self.sub_rows, self.sub_rows)

    def enter(self):
        barrier = pltpu.get_barrier_semaphore()

        def greet(peer):
            pl.semaphore_signal(barrier, inc=1, device_id={"tensor": peer}, device_id_type=MESH)

        pl.when(self.has_above)(lambda: greet(self.above))
        pl.when(self.has_below)(lambda: greet(self.below))
        greet(self.partner)
        pl.semaphore_wait(
            barrier, 1 + self.has_above.astype(jnp.int32) + self.has_below.astype(jnp.int32)
        )


class Gather:
    def __init__(self, line, source, target, sems):
        self.line, self.source, self.target = line, source, target
        self.own_sem, self.line_send, self.line_recv, self.pair_send, self.pair_recv = sems

    @staticmethod
    def scratch(chips):
        dma = pltpu.SemaphoreType.DMA
        return [
            dma((SUBS,)),
            dma((2, chips, SUBS)),
            dma((2, chips, SUBS)),
            dma((chips, SUBS)),
            dma((chips, SUBS)),
        ]

    def hop(self, way, step, sub, src, block):
        peer = self.line.above if way == 0 else self.line.below
        return remote(
            src,
            self.target.at[block, self.line.rows(sub)],
            self.line_send.at[way, step, sub],
            self.line_recv.at[way, step, sub],
            peer,
        )

    def across(self, chip, sub, src, block):
        return remote(
            src,
            self.target.at[block, self.line.rows(sub)],
            self.pair_send.at[chip, sub],
            self.pair_recv.at[chip, sub],
            self.line.partner,
        )

    def own(self, sub):
        return pltpu.make_async_copy(
            self.source.at[self.line.rows(sub)],
            self.target.at[self.line.me, self.line.rows(sub)],
            self.own_sem.at[sub],
        )

    def start(self, sub):
        line = self.line
        src = self.source.at[line.rows(sub)]
        pl.when(line.has_above)(lambda: self.hop(0, 0, sub, src, line.me).start())
        pl.when(line.has_below)(lambda: self.hop(1, 0, sub, src, line.me).start())
        self.across(line.place, sub, src, line.me).start()
        self.own(sub).start()

    def step(self, sub, step):
        line = self.line
        for way, sign in ((0, -1), (1, 1)):
            block = line.me + 2 * sign * (step + 1)
            onward = line.has_above if way == 0 else line.has_below

            @pl.when(block >= 0 if way == 0 else block < 2 * line.chips)
            def _():
                src = self.target.at[block, line.rows(sub)]
                self.hop(way, step, sub, src, block).wait_recv()
                if step + 1 < line.chips - 1:
                    pl.when(onward)(lambda: self.hop(way, step + 1, sub, src, block).start())
                self.across(block // 2, sub, src, block).start()

    def finish(self):
        line = self.line
        for sub in range(SUBS):
            src = self.source.at[line.rows(sub)]
            for chip in range(line.chips):
                copy = self.across(chip, sub, src, 2 * chip + 1 - line.core)
                copy.wait_recv()
                copy.wait_send()
            for step in range(line.chips - 1):
                sent_up = line.has_above & (line.place >= step)
                sent_down = line.has_below & (line.place + step < line.chips)
                pl.when(sent_up)(lambda: self.hop(0, step, sub, src, line.me).wait_send())
                pl.when(sent_down)(lambda: self.hop(1, step, sub, src, line.me).wait_send())
            self.own(sub).wait()


class Reduce:
    def __init__(self, line, partial, bufs, sems):
        self.line, self.partial = line, partial
        self.held, self.paired, self.from_below, self.from_above = bufs
        self.held_sem, self.pair_send, self.pair_recv, self.line_send, self.line_recv = sems

    @staticmethod
    def scratch(chips, rows, width):
        dma = pltpu.SemaphoreType.DMA
        return [pltpu.VMEM((chips, rows, width), jnp.bfloat16)] * 4 + [
            dma((chips, SUBS)),
            dma((chips, SUBS)),
            dma((chips, SUBS)),
            dma((2, chips, SUBS)),
            dma((2, chips, SUBS)),
        ]

    def load(self, chip, sub):
        rows = self.line.rows(sub)
        return pltpu.make_async_copy(
            self.partial.at[2 * chip + self.line.core, rows],
            self.held.at[chip, rows],
            self.held_sem.at[chip, sub],
        )

    def across(self, chip, sub):
        rows = self.line.rows(sub)
        return remote(
            self.partial.at[2 * chip + 1 - self.line.core, rows],
            self.paired.at[chip, rows],
            self.pair_send.at[chip, sub],
            self.pair_recv.at[chip, sub],
            self.line.partner,
        )

    def hop(self, way, chip, sub):
        rows = self.line.rows(sub)
        return remote(
            self.held.at[chip, rows],
            (self.from_below if way == 0 else self.from_above).at[chip, rows],
            self.line_send.at[way, chip, sub],
            self.line_recv.at[way, chip, sub],
            self.line.above if way == 0 else self.line.below,
        )

    def start(self):
        line = self.line
        order = []
        for step in range(line.chips):
            chip = line.chips - 1 - step // 2 if step % 2 == 0 else step // 2
            order.append(chip)
        for sub in range(SUBS):
            for chip in order:
                self.across(chip, sub).start()
                self.load(chip, sub).start()
        zeros = jnp.zeros((ROW_TILE, self.held.shape[2]), jnp.bfloat16)

        def clear(buf, chip):
            @pl.loop(0, self.held.shape[1] // ROW_TILE)
            def _(tile):
                buf[chip, pl.ds(pl.multiple_of(tile * ROW_TILE, ROW_TILE), ROW_TILE), :] = zeros

        pl.when(jnp.logical_not(line.has_below))(lambda: clear(self.from_below, 0))
        pl.when(jnp.logical_not(line.has_above))(lambda: clear(self.from_above, line.chips - 1))

    def step(self, sub, step):
        line = self.line
        for way in range(2):
            chip = line.chips - 1 - step if way == 0 else step
            arrived = self.from_below if way == 0 else self.from_above
            inner = line.has_below if way == 0 else line.has_above

            @pl.when(chip > line.place if way == 0 else chip < line.place)
            def _():
                self.load(chip, sub).wait()
                self.across(chip, sub).wait_recv()

                def add(with_arrived):
                    @pl.loop(0, line.sub_rows // ROW_TILE)
                    def _(tile):
                        at = pl.ds(
                            pl.multiple_of(sub * line.sub_rows + tile * ROW_TILE, ROW_TILE), ROW_TILE
                        )
                        total = self.held[chip, at, :].astype(jnp.float32)
                        total = total + self.paired[chip, at, :].astype(jnp.float32)
                        if with_arrived:
                            total = total + arrived[chip, at, :].astype(jnp.float32)
                        self.held[chip, at, :] = total.astype(jnp.bfloat16)

                @pl.when(inner)
                def _():
                    self.hop(way, chip, sub).wait_recv()
                    add(True)

                pl.when(jnp.logical_not(inner))(lambda: add(False))
                self.hop(way, chip, sub).start()

    def arrive(self, sub):
        line = self.line
        place = line.place
        self.load(place, sub).wait()
        self.across(place, sub).wait_recv()
        pl.when(line.has_below)(lambda: self.hop(0, place, sub).wait_recv())
        pl.when(line.has_above)(lambda: self.hop(1, place, sub).wait_recv())

    def total(self, at):
        place = self.line.place
        total = self.held[place, at, :].astype(jnp.float32)
        total = total + self.paired[place, at, :].astype(jnp.float32)
        total = total + self.from_below[place, at, :].astype(jnp.float32)
        return total + self.from_above[place, at, :].astype(jnp.float32)

    def finish(self):
        line = self.line
        for sub in range(SUBS):
            for chip in range(line.chips):
                self.across(chip, sub).wait_send()
                pl.when(chip > line.place)(lambda: self.hop(0, chip, sub).wait_send())
                pl.when(chip < line.place)(lambda: self.hop(1, chip, sub).wait_send())


def for_tiles(line, sub, body):
    @pl.loop(0, line.sub_rows // ROW_TILE)
    def _(tile):
        body(pl.ds(pl.multiple_of(sub * line.sub_rows + tile * ROW_TILE, ROW_TILE), ROW_TILE))


def run_line(line, reduce, gather, rows_done):
    steps = line.chips - 1
    line.enter()
    if reduce is not None:
        reduce.start()
    for sub in range(SUBS + 1):
        for step in range(steps):
            if reduce is not None and sub < SUBS:
                reduce.step(sub, step)
            if gather is not None and sub >= 1:
                gather.step(sub - 1, step)
        if sub < SUBS:
            if reduce is not None:
                reduce.arrive(sub)
            for_tiles(line, sub, rows_done)
            if gather is not None:
                gather.start(sub)
    if reduce is not None:
        reduce.finish()
    if gather is not None:
        gather.finish()


def unit_of(rows):
    centre = jnp.mean(rows, axis=1, keepdims=True)
    centred = rows - centre
    inv_std = lax.rsqrt(jnp.mean(centred * centred, axis=1, keepdims=True) + EPSILON)
    return centred * inv_std, inv_std


def norm_back(grad, unit, inv_std, gain):
    scaled = grad * gain
    return inv_std * (
        scaled
        - jnp.mean(scaled, axis=1, keepdims=True)
        - unit * jnp.mean(scaled * unit, axis=1, keepdims=True)
    )


def fold(rows):
    return jnp.sum(rows.reshape(-1, 8, rows.shape[1]), axis=0)


def norm_gather_kernel(chips, input_ref, gain_ref, shift_ref, whole_ref, normed_ref, *sems):
    line = Line(chips, input_ref.shape[0])
    gather = Gather(line, normed_ref, whole_ref, sems)

    def rows_done(at):
        unit, _ = unit_of(input_ref[at, :].astype(jnp.float32))
        normed_ref[at, :] = (unit * gain_ref[...] + shift_ref[...]).astype(jnp.bfloat16)

    run_line(line, None, gather, rows_done)


def branch_norm_gather_kernel(
    chips, partial_ref, input_ref, bias_ref, gain_ref, shift_ref, whole_ref, residual_ref, normed_ref, *rest
):
    line = Line(chips, input_ref.shape[0])
    reduce = Reduce(line, partial_ref, rest[:4], rest[4:9])
    gather = Gather(line, normed_ref, whole_ref, rest[9:])

    def rows_done(at):
        residual = input_ref[at, :].astype(jnp.float32) + (reduce.total(at) + bias_ref[...])
        residual_ref[at, :] = residual
        unit, _ = unit_of(residual)
        normed_ref[at, :] = (unit * gain_ref[...] + shift_ref[...]).astype(jnp.bfloat16)

    run_line(line, reduce, gather, rows_done)


def grad_gather_kernel(
    chips, partial_ref, residual_ref, grad_ref, gain_ref, whole_ref, residual_grad_ref, sums_ref, branch_ref, *rest
):
    line = Line(chips, grad_ref.shape[0])
    reduce = Reduce(line, partial_ref, rest[:4], rest[4:9])
    gather = Gather(line, branch_ref, whole_ref, rest[9:])
    sums_ref[...] = jnp.zeros_like(sums_ref)

    def rows_done(at):
        unit, inv_std = unit_of(residual_ref[at, :])
        grad = reduce.total(at)
        out_grad = grad_ref[at, :].astype(jnp.float32)
        residual_grad = out_grad + norm_back(grad, unit, inv_std, gain_ref[...])
        residual_grad_ref[at, :] = residual_grad
        branch = residual_grad.astype(jnp.bfloat16)
        branch_ref[at, :] = branch
        sums_ref[0] += fold(grad * unit)
        sums_ref[1] += fold(grad)
        sums_ref[2] += fold(branch.astype(jnp.float32))
        sums_ref[3] += fold(out_grad)

    run_line(line, reduce, gather, rows_done)


def grad_kernel(chips, partial_ref, input_ref, residual_grad_ref, gain_ref, out_ref, sums_ref, *rest):
    line = Line(chips, input_ref.shape[0])
    reduce = Reduce(line, partial_ref, rest[:4], rest[4:9])
    sums_ref[...] = jnp.zeros_like(sums_ref)

    def rows_done(at):
        unit, inv_std = unit_of(input_ref[at, :].astype(jnp.float32))
        grad = reduce.total(at)
        out_ref[at, :] = residual_grad_ref[at, :] + norm_back(grad, unit, inv_std, gain_ref[...])
        sums_ref[0] += fold(grad * unit)
        sums_ref[1] += fold(grad)

    run_line(line, reduce, None, rows_done)


def line_call(kernel, name, collective_id, operands, outs, gathers, reduces, rows, width):
    chips = lax.axis_size("tensor") // 2
    whole = jax.ShapeDtypeStruct((2 * chips, rows, width), jnp.bfloat16)
    in_vmem = pl.BlockSpec(memory_space=pltpu.VMEM)
    in_place = pl.BlockSpec(memory_space=pl.ANY)
    scratch = []
    if gathers:
        scratch.append(pltpu.VMEM((rows, width), jnp.bfloat16))
    if reduces:
        scratch += Reduce.scratch(chips, rows, width)
    if gathers:
        scratch += Gather.scratch(chips)
    return pl.pallas_call(
        functools.partial(kernel, chips),
        in_specs=([in_place] if reduces else []) + [in_vmem] * (len(operands) - int(reduces)),
        out_specs=([in_place] if gathers else []) + [in_vmem] * len(outs),
        out_shape=([whole] if gathers else []) + list(outs),
        scratch_shapes=scratch,
        compiler_params=pltpu.CompilerParams(
            collective_id=collective_id, has_side_effects=True, vmem_limit_bytes=48 * 2**20
        ),
        cost_estimate=pl.CostEstimate(
            flops=8 * rows * width * 100, bytes_accessed=100 * rows * width, transcendentals=0
        ),
        name=name,
    )(*operands)


def over_dp(grad, dimension):
    return lax.psum_scatter(
        grad.astype(jnp.bfloat16), "dp", scatter_dimension=dimension, tiled=True
    ).astype(jnp.float32)


def shards(
    layer_input,
    segment_ids,
    first_gain,
    first_shift,
    qkv_weight,
    query_value_bias,
    dense_weight,
    dense_bias,
    second_gain,
    second_shift,
    up_weight,
    up_bias,
    down_weight,
    down_bias,
    out_grad,
):
    rows, width = layer_input.shape
    ranks = lax.axis_size("tensor")
    tokens = ranks * rows
    f32_rows = jax.ShapeDtypeStruct((rows, width), jnp.float32)

    qkv_full = lax.all_gather(qkv_weight, "dp", axis=1, tiled=True)
    dense_full = lax.all_gather(dense_weight, "dp", axis=1, tiled=True)
    up_full = lax.all_gather(up_weight, "dp", axis=0, tiled=True)
    down_full = lax.all_gather(down_weight, "dp", axis=1, tiled=True)
    out_whole = lax.all_gather(out_grad, "tensor", axis=0, tiled=True)

    head_width = qkv_full.shape[2]
    up_width = up_bias.shape[0]
    qkv_cat = jnp.transpose(qkv_full, (1, 0, 2)).reshape(width, 3 * head_width)

    (whole1,) = line_call(
        norm_gather_kernel, "norm_gather", 1,
        (layer_input, first_gain[None], first_shift[None]), (), True, False, rows, width,
    )
    whole1 = whole1.reshape(tokens, width)
    zero_bias = jnp.zeros_like(query_value_bias[0])
    bias_cat = jnp.concatenate([query_value_bias[0], zero_bias, query_value_bias[1]])
    projected = (jnp.dot(whole1, qkv_cat, preferred_element_type=jnp.float32) + bias_cat).astype(
        jnp.bfloat16
    )
    head_count = head_width // HEAD_DIM
    tensor_pos = lax.axis_index("tensor")
    global_heads = tensor_pos * head_count + jnp.arange(head_count, dtype=jnp.int32)
    slopes = jnp.power(2.0, -8.0 * (global_heads + 1).astype(jnp.float32) / HEADS)
    attended, log_sums = attention_forward(projected, segment_ids, slopes)
    attn_part = jnp.dot(attended, dense_full, preferred_element_type=jnp.float32).astype(jnp.bfloat16)
    whole2, residual = line_call(
        branch_norm_gather_kernel, "branch_norm_gather", 2,
        (attn_part.reshape(ranks, rows, width), layer_input, dense_bias[None], second_gain[None], second_shift[None]),
        (f32_rows,), True, True, rows, width,
    )
    whole2 = whole2.reshape(tokens, width)
    pre_act = jnp.dot(whole2, up_full, preferred_element_type=jnp.float32) + up_bias
    activated = jax.nn.gelu(pre_act, approximate=False).astype(jnp.bfloat16)
    mlp_part = jnp.dot(activated, down_full, preferred_element_type=jnp.float32).astype(jnp.bfloat16)
    mlp_rows = lax.psum_scatter(mlp_part, "tensor", scatter_dimension=0, tiled=True)
    mlp_branch = mlp_rows.astype(jnp.float32) + down_bias
    layer_out = (residual + mlp_branch).astype(jnp.bfloat16)

    act_grad = lax.dot_general(
        out_whole, down_full, (((1,), (1,)), ((), ())), preferred_element_type=jnp.float32
    )
    unused_out, gelu_back = jax.vjp(functools.partial(jax.nn.gelu, approximate=False), pre_act)
    pre_grad = gelu_back(act_grad)[0].astype(jnp.bfloat16)
    up_bias_part = jnp.sum(pre_grad.astype(jnp.float32), axis=0)
    normed2_part = lax.dot_general(
        pre_grad, up_full, (((1,), (1,)), ((), ())), preferred_element_type=jnp.float32
    ).astype(jnp.bfloat16)
    down_grad = lax.dot_general(
        activated, out_whole, (((0,), (0,)), ((), ())), preferred_element_type=jnp.float32
    )
    down_wgrad = over_dp(down_grad, 1)
    up_grad = lax.dot_general(
        whole2, pre_grad, (((0,), (0,)), ((), ())), preferred_element_type=jnp.float32
    )
    up_wgrad = over_dp(up_grad, 0)

    branch_whole, residual_grad, second_sums = line_call(
        grad_gather_kernel, "grad_gather", 3,
        (normed2_part.reshape(ranks, rows, width), residual, out_grad, second_gain[None]),
        (f32_rows, jax.ShapeDtypeStruct((4, 8, width), jnp.float32)), True, True, rows, width,
    )
    branch_whole = branch_whole.reshape(tokens, width)
    attended_grad = lax.dot_general(
        branch_whole, dense_full, (((1,), (1,)), ((), ())), preferred_element_type=jnp.float32
    ).astype(jnp.bfloat16)
    qkv_grad_cat = attention_backward(projected, attended_grad, segment_ids, slopes, log_sums)
    dense_grad = lax.dot_general(
        attended, branch_whole, (((0,), (0,)), ((), ())), preferred_element_type=jnp.float32
    )
    dense_wgrad = over_dp(dense_grad, 1)
    qkv_sums = jnp.sum(qkv_grad_cat.astype(jnp.float32), axis=0)
    bias_part = jnp.stack([qkv_sums[:head_width], qkv_sums[2 * head_width :]])
    qkv_grad_flat = lax.dot_general(
        whole1, qkv_grad_cat, (((0,), (0,)), ((), ())), preferred_element_type=jnp.float32
    )
    qkv_grad = jnp.transpose(qkv_grad_flat.reshape(width, 3, head_width), (1, 0, 2))
    qkv_wgrad = over_dp(qkv_grad, 1)
    normed1_part = lax.dot_general(
        qkv_grad_cat, qkv_cat, (((1,), (1,)), ((), ())), preferred_element_type=jnp.float32
    ).astype(jnp.bfloat16)
    input_grad, first_sums = line_call(
        grad_kernel, "grad_rows", 4,
        (normed1_part.reshape(ranks, rows, width), layer_input, residual_grad, first_gain[None]),
        (f32_rows, jax.ShapeDtypeStruct((2, 8, width), jnp.float32)), False, True, rows, width,
    )
    early = lax.psum(jnp.sum(second_sums, axis=1), ("dp", "tensor"))
    own = lax.psum((bias_part, up_bias_part), "dp")
    late = lax.psum(jnp.sum(first_sums, axis=1), ("dp", "tensor"))
    return (
        layer_out,
        input_grad,
        late[0],
        late[1],
        qkv_wgrad,
        own[0],
        dense_wgrad,
        early[2],
        early[0],
        early[1],
        up_wgrad,
        own[1],
        down_wgrad,
        early[3],
    )


def solution(mesh):
    token_rows = P(("dp", "tensor"), None)
    placed = (
        token_rows,
        P("dp"),
        P(),
        P(),
        P(None, "dp", "tensor"),
        P(None, "tensor"),
        P("tensor", "dp"),
        P(),
        P(),
        P(),
        P("dp", "tensor"),
        P("tensor"),
        P("tensor", "dp"),
        P(),
        token_rows,
    )
    return jax.shard_map(
        shards,
        mesh=mesh,
        in_specs=placed,
        out_specs=(
            token_rows,
            token_rows,
            P(),
            P(),
            P(None, "dp", "tensor"),
            P(None, "tensor"),
            P("tensor", "dp"),
            P(),
            P(),
            P(),
            P("dp", "tensor"),
            P("tensor"),
            P("tensor", "dp"),
            P(),
        ),
        check_vma=False,
    )
```

time: 1710 us -> 901 us (0.53)
  waiting for transfers between devices: 1220 us -> 20.8 us
  Pallas kernels: 0 us -> 603 us
  local copies, waits for them, and re-layouts: 146 us -> 18.8 us
  matrix products: 221 us -> 154 us
  other arithmetic: 80 us -> 23.3 us
  blocking collectives: 0 us -> 53.6 us
    reduce_scatter x8 -> x5, waiting for transfers between devices: 661 us -> 18.3 us  [the longest x1 18.3 us: shards(): lax.psum_scatter(mlp_part, 'tensor', scatter_dimension=0, tiled=True)]
    pallas_call x0 -> x6, Pallas kernels: none -> 603 us  [the longest x4 555 us: line_call(): pl.pallas_call(functools.partial(kernel, chips), in_specs=([in_place] if...]
    all_gather x8 -> x5, waiting for transfers between devices: 426 us -> 0.05 us  [the longest x1 0.02 us: shards(): dense_full = lax.all_gather(dense_weight, 'dp', axis=1, tiled=True)]
    psum x1 -> x0, waiting for transfers between devices: 129 us -> none  [shards(): lax.psum((first_gain_part, first_shift_part, dense_bias_part, second_gain...]
    dynamic_slice x62 -> x0, local copies, waits for them, and re-layouts: 72.1 us -> none  [the longest x8 22.5 us: one_block(): lax.dynamic_slice_in_dim(value_grad, key_start, window_len, 0) + value_part]
    dot_general x36 -> x8, matrix products: 171 us -> 103 us  [the longest x1 33.1 us: shards(): lax.dot_general(out_whole, down_full, (((1,), (1,)), ((), ())), preferred...]
    psum x0 -> x2, blocking collectives: none -> 53.6 us  [the longest x1 43.4 us: shards(): late = lax.psum(jnp.sum(first_sums, axis=1), ('dp', 'tensor'))]
    dynamic_update_slice x33 -> x0, local copies, waits for them, and re-layouts: 43.1 us -> none  [the longest x8 21.8 us: one_block(): lax.dynamic_update_slice_in_dim(key_grad, lax.dynamic_slice_in_dim(key_gr...]
  transfers between devices with their start and end apart: 17 -> 10, of which waited for: 13 -> 1; matrix products, arithmetic and copies ran while one was open for 22% -> 14% of each run, Pallas kernels for 0% -> 50%
where the time goes in v1:
time: 901 us; the launch traced here: 889 us
  Pallas kernels  603 us (67%)
  matrix products  154 us (17%)
  blocking collectives  53.6 us (6%)
  other arithmetic  23.3 us (3%)
  waiting for transfers between devices  20.8 us (2%)
  local copies, waits for them, and re-layouts  18.8 us (2%)
  between operations  14.9 us (2%)
    pallas_call x4, Pallas kernels, line_call(): pl.pallas_call(functools.partial(kernel, chips), in_specs=([in_place] if...  555 us
    psum x1, blocking collectives, shards(): late = lax.psum(jnp.sum(first_sums, axis=1), ('dp', 'tensor'))  43.4 us
    dot_general x1, matrix products, shards(): lax.dot_general(out_whole, down_full, (((1,), (1,)), ((), ())), preferred...  33.1 us
    pallas_call x1, Pallas kernels, attention_backward(): pl.pallas_call(backward_kernel, grid=(seq_len // Q_BLOCK,), in_specs=[pl....  27.2 us
    pallas_call x1, Pallas kernels, attention_forward(): pl.pallas_call(forward_kernel, grid=(seq_len // Q_BLOCK,), in_specs=[pl.B...  20.9 us
    reduce_scatter x1, waiting for transfers between devices, shards(): lax.psum_scatter(mlp_part, 'tensor', scatter_dimension=0, tiled=True)  18.3 us
  transfers between devices with their start and end apart: 10, of which 1 were waited for; matrix products, arithmetic and copies ran while one was open for 14% of the time, Pallas kernels for 50%

profile of v1, /device:TPU:8, one launch (start us, length us, event | category | flops | bytes accessed | tf_op | source)
XLA Modules:
  0.0 889.1 jit_solution(11660569112979126542)
XLA Ops:
  7.2 2.3 copy.31
  9.6 0.7 all-gather.8.cloned.1.call-update
  10.4 0.7 all-gather.10.cloned.1.call-update
  11.1 0.5 all-gather.12.cloned.1.call-update
  11.7 0.5 all-gather.14.cloned.1.call-update
  12.3 1.1 copy.32.seg_col_ref
  13.3 1.6 copy-done
  14.9 0.7 copy-done.12
  15.6 0.7 copy-done.15
  16.3 74.6 %norm_gather.1 = bf16[8,256,2048]{2,1,0:T(8,128)(2,1)} custom-call(bf16[256,2048]{1,0:T(8,128)(2,1)S(1)} %copy-done, f32[1,2048]{1,0:T(1,128)S(1)} %bitcast.57, f32[1,2048]{1,0:T(1,128)S(1)} %bitcast.61), custom_call_target="tpu_custom_call" | custom-call | flops 419430400 | bytes 52428800 | tf_op jit(solution)/shard_map/norm_gather/pallas_call | solution.py:579
  91.0 10.8 %add_convert_fusion.1.proj_ref = bf16[2048,768]{1,0:T(8,128)(2,1)S(1)} fusion(f32[768]{0:T(1024)S(1)} %pad_maximum_fusion, bf16[2048,2048]{1,0:T(8,128)(2,1)} %bitcast.70, bf16[2048,768]{0,1:T(8,128)(2,1)} %bitcast.87), kind=kOutput, calls=%fused_computation.23 | convolution fusion | flops 6445596672 | bytes 14683136 | tf_op jit(solution)/shard_map/dot_general | solution.py:640
  101.9 20.9 %attention_forward.1 = (bf16[2048,256]{1,0:T(8,128)(2,1)S(1)}, f32[4,2048]{1,0:T(4,128)S(1)}) custom-call(f32[4]{0:T(128)S(1)} %multiply_power_fusion.slope_ref, bf16[2048,768]{1,0:T(8,128)(2,1)S(1)} %add_convert_fusion.1.proj_ref, s32[1,2048]{1,0:T(1,128)S(1)} %bitcast.63, s32[2048,1]{1,0:T(8,128)S(1)} %copy.32.seg_col_ref), custom_call_target="tpu_custom_call" | custom-call | flops 1610612736 | bytes 3145728 | tf_op jit(solution)/shard_map/attention_forward/pallas_call | solution.py:89
  122.8 1.7 copy-done.19
  124.5 6.9 convolution_convert_fusion.3
  131.4 216.2 %branch_norm_gather.1 = (bf16[8,256,2048]{2,1,0:T(8,128)(2,1)}, f32[256,2048]{1,0:T(8,128)S(1)}) custom-call(bf16[8,256,2048]{2,1,0:T(8,128)(2,1)} %bitcast.67, bf16[256,2048]{1,0:T(8,128)(2,1)S(1)} %copy-done.1, f32[1,2048]{1,0:T(1,128)S(1)} %bitcast.65, f32[1,2048]{1,0:T(1,128)S(1)} %bitcast.59, f32[1,2048]{1,0:T(1,128)S(1)} %bitcast.66), custom_call_target="tpu_custom_call" | custom-call | flops 419430400 | bytes 52428800 | tf_op jit(solution)/shard_map/branch_norm_gather/pallas_call | solution.py:579
  347.6 1.3 copy-done.3
  348.9 14.4 %fusion.12 = f32[2048,1024]{1,0:T(8,128)} fusion(bf16[2048,2048]{1,0:T(8,128)(2,1)} %bitcast.85, bf16[2048,1024]{1,0:T(8,128)(2,1)} %all-gather.10.cloned.1.call-done), kind=kOutput, calls=%fused_computation.38 | convolution fusion | flops 8589934592 | bytes 20971520 | tf_op jit(solution)/shard_map/dot_general | solution.py:655
  363.4 33.1 %convert_reduce_fusion = (f32[1024]{0:T(1024)S(1)}, bf16[2048,1024]{1,0:T(8,128)(2,1)S(1)}, f32[2048,1024]{1,0:T(8,128)}) fusion(f32[2048,1024]{1,0:T(8,128)} %fusion.12, f32[1024]{0:T(1024)S(1)} %copy-done.22, bf16[2048,2048]{1,0:T(8,128)(2,1)} %all-gather.14.cloned.1.call-done, bf16[1024,2048]{1,0:T(8,128)(2,1)} %all-gather.12.cloned.1.call-done), kind=kOutput, calls=%fused_computation.2 | convolution fusion | flops 8747219968 | bytes 33562624 | tf_op jit(solution)/shard_map/dot_general | solution.py:662
  396.5 11.4 %convolution_convert_fusion.1 = bf16[2048,2048]{1,0:T(8,128)(2,1)} fusion(bf16[2048,1024]{1,0:T(8,128)(2,1)S(1)} %get-tuple-element.37, bf16[2048,1024]{1,0:T(8,128)(2,1)S(1)} %copy-done.24), kind=kOutput, calls=%fused_computation.19 | convolution fusion | flops 8594128896 | bytes 16777216 | tf_op jit(solution)/shard_map/dot_general | solution.py:668
  407.9 161.4 %grad_gather.1 = (bf16[8,256,2048]{2,1,0:T(8,128)(2,1)}, f32[256,2048]{1,0:T(8,128)S(1)}, f32[4,8,2048]{2,1,0:T(8,128)S(1)}) custom-call(bf16[8,256,2048]{2,1,0:T(8,128)(2,1)} %bitcast.72, f32[256,2048]{1,0:T(8,128)S(1)} %copy-done.4, bf16[256,2048]{1,0:T(8,128)(2,1)S(1)} %copy-done.6, f32[1,2048]{1,0:T(1,128)S(1)} %bitcast.60), custom_call_target="tpu_custom_call" | custom-call | flops 419430400 | bytes 52428800 | tf_op jit(solution)/shard_map/grad_gather/pallas_call | solution.py:579
  569.3 1.3 copy-done.7
  570.6 6.8 convolution_convert_fusion.7
  577.4 0.0 reduce-scatter.8.cloned.1.call-start
  577.5 5.9 convolution_convert_fusion.8.grad_ref
  583.4 27.2 %attention_backward.1 = bf16[2048,768]{1,0:T(8,128)(2,1)S(1)} custom-call(f32[4]{0:T(128)S(1)} %multiply_power_fusion.slope_ref, bf16[2048,768]{1,0:T(8,128)(2,1)} %copy-done.19, bf16[2048,256]{1,0:T(8,128)(2,1)S(1)} %convolution_convert_fusion.8.grad_ref, f32[4,2048]{1,0:T(4,128)S(1)} %get-tuple-element.27.lse_ref, s32[1,2048]{1,0:T(1,128)S(1)} %bitcast.64, ...), custom_call_target="tpu_custom_call" | custom-call | flops 4026531840 | bytes 7340032 | tf_op jit(solution)/shard_map/attention_backward/pallas_call | solution.py:181
  610.5 3.0 copy.34
  613.5 11.3 %fusion.6 = bf16[3,2048,256]{2,1,0:T(8,128)(2,1)} fusion(bf16[2048,2048,1]{1,0,2:T(8,128)(2,1)} %bitcast.71, bf16[3,256,2048]{2,1,0:T(8,128)(2,1)} %bitcast.74), kind=kOutput, calls=%fused_computation.27 | convolution fusion | flops 6444023808 | bytes 14680064 | tf_op jit(solution)/shard_map/dot_general | solution.py:696
  624.8 0.0 reduce-scatter.12.cloned.1.call-start
  624.9 14.0 %convolution_convert_fusion.5 = bf16[2048,1024]{1,0:T(8,128)(2,1)} fusion(bf16[2048,2048]{1,0:T(8,128)(2,1)} %bitcast.86, bf16[2048,1024]{1,0:T(8,128)(2,1)} %copy-done.25), kind=kOutput, calls=%fused_computation.25 | convolution fusion | flops 8592031744 | bytes 16777216 | tf_op jit(solution)/shard_map/dot_general | solution.py:675
  638.9 0.3 reduce-scatter.14.cloned.1.call-start
  639.2 10.3 %multiply_convert_fusion = bf16[2048,1024]{1,0:T(8,128)(2,1)} fusion(f32[2048,1024]{1,0:T(8,128)} %get-tuple-element.38, f32[2048,1024]{1,0:T(8,128)} %fusion.12, f32[1024]{0:T(1024)S(1)} %copy-done.22), kind=kLoop, calls=%fused_computation.4 | loop fusion | flops 8388608 | bytes 20975616 | tf_op jit(solution)/shard_map/convert_element_type | solution.py:656
  649.5 14.1 %convolution_convert_fusion.4 = bf16[1024,2048]{1,0:T(8,128)(2,1)} fusion(bf16[2048,1024]{1,0:T(8,128)(2,1)} %multiply_convert_fusion, bf16[2048,2048]{1,0:T(8,128)(2,1)} %all-gather.14.cloned.1.call-done), kind=kOutput, calls=%fused_computation.24 | convolution fusion | flops 8592031744 | bytes 16777216 | tf_op jit(solution)/shard_map/dot_general | solution.py:671
  663.7 14.0 %convolution_convert_fusion.2 = bf16[2048,2048]{1,0:T(8,128)(2,1)} fusion(bf16[2048,1024]{1,0:T(8,128)(2,1)} %multiply_convert_fusion, bf16[1024,2048]{1,0:T(8,128)(2,1)} %all-gather.12.cloned.1.call-done), kind=kOutput, calls=%fused_computation.20 | convolution fusion | flops 8594128896 | bytes 16777216 | tf_op jit(solution)/shard_map/dot_general | solution.py:657
  677.8 0.1 reduce_sum.38
  677.9 10.8 %convolution_convert_fusion = bf16[2048,2048]{1,0:T(8,128)(2,1)} fusion(bf16[2048,768]{1,0:T(8,128)(2,1)S(1)} %attention_backward.1, bf16[2048,768]{0,1:T(8,128)(2,1)} %bitcast.88), kind=kOutput, calls=%fused_computation.18 | convolution fusion | flops 6446645248 | bytes 14680064 | tf_op jit(solution)/shard_map/dot_general | solution.py:701
  688.7 103.2 %grad_rows.1 = (f32[256,2048]{1,0:T(8,128)S(1)}, f32[2,8,2048]{2,1,0:T(8,128)S(1)}) custom-call(bf16[8,256,2048]{2,1,0:T(8,128)(2,1)} %bitcast.73, bf16[256,2048]{1,0:T(8,128)(2,1)S(1)} %copy-done.2, f32[256,2048]{1,0:T(8,128)S(1)} %copy-done.8, f32[1,2048]{1,0:T(1,128)S(1)} %bitcast.58), custom_call_target="tpu_custom_call" | custom-call | flops 419430400 | bytes 52428800 | tf_op jit(solution)/shard_map/grad_rows/pallas_call | solution.py:579
  792.0 1.3 copy-done.9
  793.3 0.5 convert_reduce_fusion.1
  793.8 10.2 %all-reduce.1 = (f32[2,256]{1,0:T(2,128)}, f32[1024]{0:T(1024)}) all-reduce(f32[2,256]{1,0:T(2,128)S(1)} %pad_maximum_fusion.1, f32[1024]{0:T(1024)S(1)} %get-tuple-element.36), channel_id=1, replica_groups=mesh['dp'=4,'tensor'=8] {'dp'}, use_global_device_ids=true, to_apply=%region_5.0 | all-reduce | flops 1536 | bytes 12288 | tf_op jit(solution)/shard_map/psum | solution.py:710
  804.0 43.4 %all-reduce = (f32[2,2048]{1,0:T(2,128)S(1)}, f32[4,2048]{1,0:T(4,128)S(1)}) all-reduce(f32[2,2048]{1,0:T(2,128)S(1)} %reduce_sum.36, f32[4,2048]{1,0:T(4,128)S(1)} %reduce_sum.38), channel_id=1, replica_groups=mesh['dp'=4,'tensor'=8] {'dp','tensor'}, use_global_device_ids=true, to_apply=%region_2.0 | all-reduce | flops 12288 | bytes 98304 | tf_op jit(solution)/shard_map/psum | solution.py:711
  847.4 0.6 fusion.8
  848.1 1.8 convert_element_type.82
  849.9 2.4 convert_element_type.79
  852.3 2.8 convert_element_type.84
  855.1 2.8 convert_element_type.87
  857.9 18.3 %reduce-scatter.6.cloned.1.call-done = bf16[256,2048]{1,0:T(8,128)(2,1)} async-done(((bf16[2048,2048]{1,0:T(8,128)(2,1)}), bf16[256,2048]{1,0:T(8,128)(2,1)}) %reduce-scatter.6.cloned.1.call-update) | async-done | bytes 1048592 | tf_op jit(solution)/shard_map/reduce_scatter | solution.py:658
  876.2 2.5 add_convert_fusion.2
  878.7 3.1 copy.39
  (74 shorter events, 0.6 us)
Async XLA Ops:
  7.2 83.8 %copy-start.23 = (f32[2,256]{1,0:T(2,128)S(1)}, f32[2,256]{1,0:T(2,128)}, u32[]{:S(2)}) copy-start(f32[2,256]{1,0:T(2,128)} %param.20) | copy-start | bytes 6148
  7.2 83.8 %all-gather.6.cloned.1.call-start = ((), (), s32[]{:S(2)}) async-start(), calls=%async_computation.5 | async-start | bytes 3932160 | tf_op jit(solution)/shard_map/all_gather | solution.py:623
  9.6 114.9 %all-gather.8.cloned.1.call-start = ((), (), s32[]{:S(2)}) async-start(), calls=%async_computation.6 | async-start | bytes 1310720 | tf_op jit(solution)/shard_map/all_gather | solution.py:624
  10.3 338.6 %all-gather.10.cloned.1.call-start = ((), (), s32[]{:S(2)}) async-start(), calls=%async_computation.7 | async-start | bytes 5242880 | tf_op jit(solution)/shard_map/all_gather | solution.py:625
  11.0 352.3 %all-gather.12.cloned.1.call-start = ((), (), s32[]{:S(2)}) async-start(), calls=%async_computation.8 | async-start | bytes 5242880 | tf_op jit(solution)/shard_map/all_gather | solution.py:626
  11.6 351.7 %all-gather.14.cloned.1.call-start = ((), (), s32[]{:S(2)}) async-start(), calls=%async_computation.10 | async-start | bytes 9437184 | tf_op jit(solution)/shard_map/all_gather | solution.py:627
  12.2 835.9 %reduce-scatter.10.cloned.1.call-start = ((), (), s32[]{:S(2)}) async-start(), calls=%async_computation.12 | async-start | bytes 1310720 | tf_op jit(solution)/shard_map/reduce_scatter | solution.py:596
  13.3 88.6 %copy-start.10 = (s32[2048,1]{1,0:T(8,128)}, s32[2048,1]{1,0:T(8,128)S(1)}, u32[]{:S(2)}) copy-start(s32[2048,1]{1,0:T(8,128)S(1)} %copy.32.seg_col_ref) | copy-start | bytes 24580
  13.3 1.6 copy-start
  14.9 0.7 copy-start.12
  15.6 0.7 copy-start.15
  91.0 10.9 %copy-start.16 = (s32[2048]{0:T(1024)S(1)}, s32[2048]{0:T(1024)}, u32[]{:S(2)}) copy-start(s32[2048]{0:T(1024)} %param.16) | copy-start | bytes 24580
  122.8 1.7 copy-start.19
  124.5 6.9 copy-start.1
  124.5 6.9 copy-start.14
  124.5 6.9 copy-start.17
  124.5 6.9 copy-start.18
  347.6 1.3 copy-start.3
  348.9 14.4 %copy-start.22 = (f32[1024]{0:T(1024)S(1)}, f32[1024]{0:T(1024)}, u32[]{:S(2)}) copy-start(f32[1024]{0:T(1024)} %param.26) | copy-start | bytes 12292
  363.4 33.1 %copy-start.24 = (bf16[2048,1024]{1,0:T(8,128)(2,1)S(1)}, bf16[2048,1024]{1,0:T(8,128)(2,1)}, u32[]{:S(2)}) copy-start(bf16[2048,1024]{1,0:T(8,128)(2,1)} %all-gather.10.cloned.1.call-done) | copy-start | bytes 12582916
  396.5 11.4 %copy-start.25 = (bf16[2048,1024]{1,0:T(8,128)(2,1)}, bf16[2048,1024]{1,0:T(8,128)(2,1)S(1)}, u32[]{:S(2)}) copy-start(bf16[2048,1024]{1,0:T(8,128)(2,1)S(1)} %get-tuple-element.37) | copy-start | bytes 12582916
  396.5 11.4 %copy-start.4 = (f32[256,2048]{1,0:T(8,128)S(1)}, f32[256,2048]{1,0:T(8,128)}, u32[]{:S(2)}) copy-start(f32[256,2048]{1,0:T(8,128)} %copy-done.3) | copy-start | bytes 6291460
  396.5 11.4 %copy-start.6 = (bf16[256,2048]{1,0:T(8,128)(2,1)S(1)}, bf16[256,2048]{1,0:T(8,128)(2,1)}, u32[]{:S(2)}) copy-start(bf16[256,2048]{1,0:T(8,128)(2,1)} %grad_ref.1) | copy-start | bytes 3145732
  569.3 1.3 copy-start.7
  570.6 6.9 copy-start.20
  577.4 272.5 %reduce-scatter.8.cloned.1.call-start = ((), (), s32[]{:S(2)}) async-start(), calls=%async_computation.11 | async-start | bytes 3932160 | tf_op jit(solution)/shard_map/reduce_scatter | solution.py:596
  577.5 5.9 copy-start.11
  624.8 227.5 %reduce-scatter.12.cloned.1.call-start = ((), (), s32[]{:S(2)}) async-start(), calls=%async_computation.13 | async-start | bytes 5242880 | tf_op jit(solution)/shard_map/reduce_scatter | solution.py:596
  638.9 216.2 %reduce-scatter.14.cloned.1.call-start = ((), (), s32[]{:S(2)}) async-start(), calls=%async_computation.14 | async-start | bytes 5242880 | tf_op jit(solution)/shard_map/reduce_scatter | solution.py:596
  663.7 212.5 %reduce-scatter.6.cloned.1.call-start = ((), (), s32[]{:S(2)}) async-start(), calls=%async_computation.9 | async-start | bytes 9437184 | tf_op jit(solution)/shard_map/reduce_scatter | solution.py:658
  677.8 10.9 %copy-start.2 = (bf16[256,2048]{1,0:T(8,128)(2,1)S(1)}, bf16[256,2048]{1,0:T(8,128)(2,1)}, u32[]{:S(2)}) copy-start(bf16[256,2048]{1,0:T(8,128)(2,1)} %input_ref.5) | copy-start | bytes 3145732
  677.9 10.9 %copy-start.8 = (f32[256,2048]{1,0:T(8,128)S(1)}, f32[256,2048]{1,0:T(8,128)}, u32[]{:S(2)}) copy-start(f32[256,2048]{1,0:T(8,128)} %copy-done.7) | copy-start | bytes 6291460
  677.9 10.9 %copy-start.13 = (f32[2048]{0:T(1024)S(1)}, f32[2048]{0:T(1024)}, u32[]{:S(2)}) copy-start(f32[2048]{0:T(1024)} %param.17) | copy-start | bytes 24580
  792.0 1.3 copy-start.9
  793.3 82.9 %copy-start.21 = (f32[2048]{0:T(1024)S(1)}, f32[2048]{0:T(1024)}, u32[]{:S(2)}) copy-start(f32[2048]{0:T(1024)} %param.28) | copy-start | bytes 24580
  793.8 82.4 %copy-start.5 = (f32[256,2048]{1,0:T(8,128)S(1)}, f32[256,2048]{1,0:T(8,128)}, u32[]{:S(2)}) copy-start(f32[256,2048]{1,0:T(8,128)} %copy-done.3) | copy-start | bytes 6291460
Sparse Core Ops, SparseCore 0:
  10.4 44.8 all-gather.5
  57.1 26.3 all-gather.7
  85.4 52.5 all-gather.9
  139.7 52.4 all-gather.11
  193.6 97.2 all-gather.13
  577.5 33.6 reduce-scatter.9
  625.0 49.7 reduce-scatter.7
  677.7 52.5 reduce-scatter.11
  733.3 52.5 reduce-scatter.13
  788.1 88.0 reduce-scatter.5
